TPU v7x, 32 devices: a whole 2x2x4 slice. The times are simulated.
32 devices in a mesh: dp: 2 (over core), seq: 16 (over z, y, x).
Axes of the slice: x: 2, y: 2, z: 4, core: 2. Of those that a mesh axis runs over, the one named last changes fastest.
Arguments:
- latent: bfloat16 [32, 1024, 1152], P(('dp', 'seq')), parts along dimension 0, may hold values from -6 to 6
- w_qkv_space: bfloat16 [1152, 1728], replicated, may hold values from -0.1875 to 0.1875
- w_out_space: bfloat16 [576, 1152], replicated, may hold values from -0.25 to 0.25
- w_qkv_time: bfloat16 [1152, 1728], replicated, may hold values from -0.1875 to 0.1875
- w_out_time: bfloat16 [576, 1152], replicated, may hold values from -0.25 to 0.25
- modulation: float32 [12, 1152], P('dp'), parts along dimension 0, may hold values from -1.5 to 5
Outputs:
- block_out: bfloat16 [32, 1024, 1152], P(('dp', 'seq')), parts along dimension 0
There are 2 independent parts, one for each index of `dp`. A program takes and returns all parts, laid end to end along the dimension named above; an argument that names none is the same for every part. Nothing has to cross between parts.
All inputs are finite; a program needn't handle non-finite values.
Results may differ from a plain program's by a relative error of at most 0.02.
The roundings to bfloat16 on the way count: a program that leaves them out, or rounds other values in their place, can miss the bound.
Values may be sent and summed in bfloat16 or wider, within the bound.
A program may use at most 128 MiB of HBM per device.

v0:
```python
import jax
import jax.numpy as jnp
from jax import lax
from jax.sharding import PartitionSpec as P

HEADS = 8
HEAD_DIM = 72


EPS = 1e-06


def normalize(values):
    center = jnp.mean(values, -1, keepdims=True)
    centred = values - center
    spread = jnp.mean(centred * centred, -1, keepdims=True)
    return centred * lax.rsqrt(spread + EPS)


def modulated(latent, modulation, first):
    normed = normalize(latent.astype(jnp.float32))
    return (normed * (1.0 + modulation[first + 1]) + modulation[first]).astype(jnp.bfloat16)


def softmax_weights(scores, axis):
    top_score = jnp.max(scores, axis, keepdims=True)
    expo = jnp.exp(scores - top_score)
    return (expo / jnp.sum(expo, axis, keepdims=True)).astype(jnp.bfloat16)


def attend_space(frame_rows, w_qkv, w_out, modulation):
    tokens_here = frame_rows.shape[0]
    mixed = modulated(frame_rows, modulation, 0)
    triple = jnp.dot(mixed, w_qkv, preferred_element_type=jnp.float32).astype(jnp.bfloat16)
    triple = triple.reshape(tokens_here, 3, HEADS, HEAD_DIM)
    factor = 1.0 / float(HEAD_DIM) ** 0.5
    scores = (
        jnp.einsum("shd,thd->hst", triple[:, 0], triple[:, 1], preferred_element_type=jnp.float32)
        * factor
    )
    weights = softmax_weights(scores, 2)
    outputs = jnp.einsum(
        "hst,thd->shd", weights, triple[:, 2], preferred_element_type=jnp.float32
    ).astype(jnp.bfloat16)
    delta = jnp.dot(
        outputs.reshape(tokens_here, HEADS * HEAD_DIM), w_out, preferred_element_type=jnp.float32
    )
    return (frame_rows.astype(jnp.float32) + modulation[2] * delta).astype(jnp.bfloat16)


def attend_time(queries, key_heads, value_heads):
    factor = 1.0 / float(queries.shape[-1]) ** 0.5
    scores = (
        jnp.einsum("fphd,gphd->phfg", queries, key_heads, preferred_element_type=jnp.float32)
        * factor
    )
    weights = softmax_weights(scores, 3)
    return jnp.einsum(
        "phfg,gphd->fphd", weights, value_heads, preferred_element_type=jnp.float32
    ).astype(jnp.bfloat16)


def shards(latent, w_qkv_space, w_out_space, w_qkv_time, w_out_time, modulation):
    after_space = attend_space(latent[0], w_qkv_space, w_out_space, modulation)
    spatial, width = after_space.shape
    patches = lax.all_to_all(after_space[None], "seq", split_axis=1, concat_axis=0, tiled=True)
    frames, positions, width = patches.shape
    mixed = modulated(patches, modulation, 3).reshape(frames * positions, width)
    triple = jnp.dot(mixed, w_qkv_time, preferred_element_type=jnp.float32).astype(jnp.bfloat16)
    triple = triple.reshape(frames, positions, 3, HEADS, HEAD_DIM)
    outputs = attend_time(triple[:, :, 0], triple[:, :, 1], triple[:, :, 2])
    delta = jnp.dot(
        outputs.reshape(frames * positions, HEADS * HEAD_DIM),
        w_out_time,
        preferred_element_type=jnp.float32,
    )
    result = patches.astype(jnp.float32).reshape(frames * positions, width) + modulation[5] * delta
    result = result.astype(jnp.bfloat16).reshape(frames, positions, width)
    return lax.all_to_all(result, "seq", split_axis=0, concat_axis=1, tiled=True)


def solution(mesh):
    in_specs = (P(("dp", "seq"), None, None), P(), P(), P(), P(), P("dp", None))
    out_specs = P(("dp", "seq"), None, None)
    return jax.shard_map(shards, mesh=mesh, in_specs=in_specs, out_specs=out_specs, check_vma=False)
```

profile of v0, /device:TPU:0, one launch (start us, length us, event | category | flops | bytes accessed | tf_op | source)
XLA Modules:
  0.0 269.0 jit_solution(783976993422969830)
XLA Ops:
  1.2 2.1 convert_reduce_fusion.1
  4.0 9.2 %convolution_convert_fusion.1 = bf16[1024,1728]{0,1:T(8,128)(2,1)} fusion(bf16[1152,1728]{0,1:T(8,128)(2,1)} %param.7, bf16[1,1024,1152]{2,1,0:T(8,128)(2,1)S(1)} %copy-done.2, f32[1152]{0:T(1024)S(1)} %get-tuple-element.6, f32[1152]{0:T(1024)S(1)} %get-tuple-element.7, f32[1024]{0:T(1024)S(1)} %add_rsqrt_fusion.1, f32[1024]{0:T(1024)S(1)} %broadcast_multiply_fusion.1), kind=kOutput, calls=%fused_computation.36 | convolution fusion | flops 4085710848 | bytes 9896960 | tf_op jit(solution)/shard_map/dot_general | solution.py:34
  13.2 17.8 %fusion.55 = (f32[8,1024]{1,0:T(8,128)S(1)}, f32[8,1024,1024]{1,2,0:T(8,128)}) fusion(bf16[1024,3,8,72]{0,3,2,1:T(8,128)(2,1)} %bitcast.104), kind=kOutput, calls=%fused_computation.75 | convolution fusion | flops 1233126400 | bytes 35946496 | tf_op jit(solution)/shard_map/sub | solution.py:27
  31.1 12.8 %fusion.50 = bf16[8,72,1024]{2,1,0:T(8,128)(2,1)S(1)} fusion(f32[8,1024,1024]{1,2,0:T(8,128)} %get-tuple-element.17, f32[8,1024]{1,0:T(8,128)S(1)} %get-tuple-element.16, bf16[1024,3,8,72]{0,3,2,1:T(8,128)(2,1)} %bitcast.105), kind=kOutput, calls=%fused_computation.57 | convolution fusion | flops 1225326592 | bytes 35946496 | tf_op jit(solution)/shard_map/hst,thd->shd/dot_general | solution.py:42
  43.9 2.4 fusion.26
  46.3 5.8 %copy.37 = bf16[1,1024,1152]{2,0,1:T(2,128)(2,1)} copy(bf16[1,1024,1152]{2,1,0:T(8,128)(2,1)S(1)} %fusion.26) | data formatting | bytes 4718592 | tf_op jit(solution)/shard_map/broadcast_in_dim | solution.py:66
  52.6 16.3 %reduce.15 = bf16[1024,1152]{1,0:T(8,128)(2,1)} reduce(bf16[1024,1,1152]{2,1,0:T(2,128)(2,1)} %bitcast.100, bf16[]{:T(256)} %broadcast.73), dimensions={1}, to_apply=%bitcast.99.reduce_sub_computation | reduce | bytes 4718594
  68.9 4.1 %reshape.90 = bf16[16,2,36864]{2,1,0:T(2,128)(2,1)} reshape(bf16[1024,1152]{1,0:T(8,128)(2,1)} %reduce.15) | data formatting | bytes 4718592
  73.0 63.4 %all_to_all.21 = bf16[16,2,36864]{2,1,0:T(2,128)(2,1)} all-to-all(bf16[16,2,36864]{2,1,0:T(2,128)(2,1)} %reshape.90), channel_id=1, replica_groups=mesh['dp'=2,'seq'=16] {'seq'}, dimensions={0} | all-to-all | bytes 4718592 | tf_op jit(solution)/shard_map/all_to_all | solution.py:66
  136.4 10.7 %reshape.91 = bf16[1024,1,1152]{2,1,0:T(2,128)(2,1)} reshape(bf16[16,2,36864]{2,1,0:T(2,128)(2,1)} %all_to_all.21) | data formatting | bytes 4718592
  147.1 2.9 %convert_reduce_fusion = (f32[1024]{0:T(1024)S(1)}, bf16[1,1024,1152]{2,1,0:T(8,128)(2,1)S(1)}) fusion(bf16[1,1024,1152]{2,0,1:T(2,128)(2,1)} %bitcast.101), kind=kLoop, calls=%fused_computation.9 | loop fusion | flops 2358272 | bytes 4722688 | tf_op jit(solution)/shard_map/reduce_sum | solution.py:14
  151.5 7.1 %convolution_convert_fusion = bf16[1024,1728]{0,1:T(8,128)(2,1)} fusion(bf16[1152,1728]{0,1:T(8,128)(2,1)S(1)} %copy-done.4, bf16[1,1024,1152]{2,1,0:T(8,128)(2,1)S(1)} %get-tuple-element.12, f32[1152]{0:T(1024)S(1)} %get-tuple-element.9, f32[1152]{0:T(1024)S(1)} %get-tuple-element.10, f32[1024]{0:T(1024)S(1)} %add_rsqrt_fusion, ...), kind=kOutput, calls=%fused_computation.35 | convolution fusion | flops 4085710848 | bytes 9896960 | tf_op jit(solution)/shard_map/dot_general | solution.py:69
  158.6 9.9 %reshape.83 = bf16[16,64,3,8,72]{1,0,4,3,2:T(8,128)(2,1)} reshape(bf16[1024,1728]{0,1:T(8,128)(2,1)} %convolution_convert_fusion) | data formatting | bytes 7077888 | tf_op jit(solution)/shard_map/reshape | solution.py:70
  168.5 6.7 %fusion.54 = (bf16[16,64,1,8,72]{1,0,4,3,2:T(8,128)(2,1)}, bf16[16,64,1,8,72]{1,0,4,3,2:T(8,128)(2,1)}, bf16[16,64,1,8,72]{1,0,4,3,2:T(8,128)(2,1)}) fusion(bf16[16,64,3,8,72]{1,0,4,3,2:T(8,128)(2,1)} %reshape.83), kind=kLoop, calls=%fused_computation.74 | loop fusion | bytes 7077888 | tf_op jit(solution)/shard_map/slice | solution.py:71
  175.3 5.4 %copy.33 = bf16[16,64,1,8,72]{4,0,3,1,2:T(8,128)(2,1)S(1)} copy(bf16[16,64,1,8,72]{1,0,4,3,2:T(8,128)(2,1)} %get-tuple-element.14) | data formatting | bytes 2359296
  180.6 6.3 %copy.34 = bf16[16,64,1,8,72]{4,0,3,1,2:T(8,128)(2,1)} copy(bf16[16,64,1,8,72]{1,0,4,3,2:T(8,128)(2,1)} %get-tuple-element.15) | data formatting | bytes 2359296
  186.9 2.8 %fusion.42 = f32[64,8,16,16]{2,3,1,0:T(8,128)S(1)} fusion(bf16[16,64,1,8,72]{4,0,3,1,2:T(8,128)(2,1)} %copy.34, bf16[16,64,1,8,72]{4,0,3,1,2:T(8,128)(2,1)S(1)} %copy.33), kind=kOutput, calls=%fused_computation.50 | convolution fusion | flops 18874368 | bytes 2883584 | tf_op jit(solution)/shard_map/fphd,gphd->phfg/dot_general | solution.py:54
  189.7 4.2 %fusion.56 = (f32[64,8,16]{2,1,0:T(8,128)}, f32[64,8,16,16]{2,3,1,0:T(8,128)}) fusion(f32[64,8,16,16]{2,3,1,0:T(8,128)S(1)} %fusion.42), kind=kOutput, calls=%fused_computation.76 | output fusion | flops 524303 | bytes 1081344 | tf_op jit(solution)/shard_map/sub | solution.py:27
  193.9 5.4 %copy.32 = bf16[16,64,1,8,72]{4,0,3,1,2:T(8,128)(2,1)S(1)} copy(bf16[16,64,1,8,72]{1,0,4,3,2:T(8,128)(2,1)} %get-tuple-element.13) | data formatting | bytes 2359296
  199.3 3.1 %convert_bitcast_fusion.2 = bf16[16,64,8,72]{3,0,2,1:T(8,128)(2,1)S(1)} fusion(f32[64,8,16,16]{2,3,1,0:T(8,128)} %get-tuple-element.19, f32[64,8,16]{2,1,0:T(8,128)} %get-tuple-element.18, bf16[16,64,1,8,72]{4,0,3,1,2:T(8,128)(2,1)S(1)} %copy.32), kind=kOutput, calls=%fused_computation.54 | convolution fusion | flops 19726336 | bytes 2916352 | tf_op jit(solution)/shard_map/phfg,gphd->fphd/dot_general | solution.py:58
  202.9 2.5 reshape.80
  205.4 4.6 %fusion.22 = bf16[1024,1152]{1,0:T(8,128)(2,1)S(1)} fusion(bf16[1,1024,1152]{2,1,0:T(8,128)(2,1)} %copy-done.1, bf16[1024,576]{1,0:T(8,128)(2,1)} %reshape.80, bf16[576,1152]{1,0:T(8,128)(2,1)} %param.10, f32[1152]{0:T(1024)S(1)} %get-tuple-element.5), kind=kOutput, calls=%fused_computation.30 | convolution fusion | flops 1363673088 | bytes 7229952 | tf_op jit(solution)/shard_map/dot_general | solution.py:72
  210.0 57.6 %all_to_all.22 = bf16[16,64,1152]{2,1,0:T(8,128)(2,1)S(1)} all-to-all(bf16[16,64,1152]{2,1,0:T(8,128)(2,1)S(1)} %bitcast.103), channel_id=1, replica_groups=mesh['dp'=2,'seq'=16] {'seq'}, dimensions={0} | all-to-all | bytes 4718592 | tf_op jit(solution)/shard_map/all_to_all | solution.py:79
  267.6 1.4 copy.39
  (19 shorter events, 4.3 us)
Async XLA Ops:
  0.0 43.9 %copy-start = (bf16[576,1152]{1,0:T(8,128)(2,1)S(1)}, bf16[576,1152]{1,0:T(8,128)(2,1)}, u32[]{:S(2)}) copy-start(bf16[576,1152]{1,0:T(8,128)(2,1)} %param.8) | copy-start | bytes 3981316
  0.0 3.3 %copy-start.2 = (bf16[1,1024,1152]{2,1,0:T(8,128)(2,1)S(1)}, bf16[1,1024,1152]{2,1,0:T(8,128)(2,1)}, u32[]{:S(2)}) copy-start(bf16[1,1024,1152]{2,1,0:T(8,128)(2,1)} %param.6) | copy-start | bytes 7077892
  31.0 12.9 %copy-start.3 = (bf16[1,1024,1152]{2,1,0:T(8,128)(2,1)S(1)}, bf16[1,1024,1152]{2,1,0:T(8,128)(2,1)}, u32[]{:S(2)}) copy-start(bf16[1,1024,1152]{2,1,0:T(8,128)(2,1)} %param.6) | copy-start | bytes 7077892
  147.1 4.3 %copy-start.4 = (bf16[1152,1728]{0,1:T(8,128)(2,1)S(1)}, bf16[1152,1728]{0,1:T(8,128)(2,1)}, u32[]{:S(2)}) copy-start(bf16[1152,1728]{0,1:T(8,128)(2,1)} %param.9) | copy-start | bytes 11943940
  150.0 1.4 copy-start.1
where the time goes:
time: 270 us; the launch traced here: 269 us
  blocking collectives  121 us (45%)
  local copies, waits for them, and re-layouts  59.8 us (22%)
  matrix products  59.8 us (22%)
  other arithmetic  28.2 us (10%)
    all_to_all x1, blocking collectives, shards(): lax.all_to_all(after_space[None], 'seq', split_axis=1, concat_axis=0, til...  63.4 us
    all_to_all x1, blocking collectives, shards(): lax.all_to_all(result, 'seq', split_axis=0, concat_axis=1, tiled=True)  57.6 us
    unnamed x17, local copies, waits for them, and re-layouts  34.3 us
    sub x1, matrix products, softmax_weights(): expo = jnp.exp(scores - top_score)  17.8 us
    unnamed x1, other arithmetic  16.3 us
    dot_general x1, matrix products, attend_space(): jnp.einsum('hst,thd->shd', weights, triple[:, 2], preferred_element_type=...  12.8 us
    reshape x1, local copies, waits for them, and re-layouts, shards(): triple = triple.reshape(frames, positions, 3, HEADS, HEAD_DIM)  9.93 us
    dot_general x1, matrix products, attend_space(): jnp.dot(mixed, w_qkv, preferred_element_type=jnp.float32)  9.17 us

commit v1 on v0

v1 whole, which is shorter than its diff:
```python
import functools

import jax
import jax.numpy as jnp
from jax import lax
from jax.experimental import pallas as pl
from jax.experimental.pallas import tpu as pltpu
from jax.sharding import PartitionSpec as P

HEADS = 8
HEAD_DIM = 72
EPS = 1e-06
LANES = 128
TILE = 256
GROUP = 16
LOG2E = 1.4426950408889634
FAR = -1e30

f32, bf16 = jnp.float32, jnp.bfloat16


def modulated(rows, shift, scale):
    center = jnp.mean(rows, -1, keepdims=True)
    centred = rows - center
    spread = jnp.mean(centred * centred, -1, keepdims=True)
    return (centred * lax.rsqrt(spread + EPS) * (1.0 + scale) + shift).astype(bf16)


def windows(padded):
    out = []
    for head in range(HEADS):
        start = head * HEAD_DIM
        base = start // LANES * LANES
        wide = LANES if start + HEAD_DIM <= base + LANES else 2 * LANES
        base = min(base, padded - wide)
        out.append((base, wide, start - base))
    return out


def kernel(
    n, latent_hbm, wqs_hbm, wos_hbm, wqt_hbm, wot_hbm, mod, out_hbm,
    lat, wqs, wos, wqt, wot, q, k, v, attn, after, recv, bias, back_send, back_recv, out,
    load_sem, store_sem, send_sem, recv_sem, bsend_sem, brecv_sem,
):
    me = lax.axis_index("seq")
    tokens, width = lat.shape
    pos = tokens // n
    hd = HEADS * HEAD_DIM
    padded = q.shape[2]
    per = TILE // pos
    blocks = tokens // TILE
    half = blocks // 2
    groups = pos // GROUP
    keys = n * GROUP
    mine = me // per
    side, place = mine // half, mine % half
    factor = LOG2E / float(HEAD_DIM) ** 0.5

    def block_at(step):
        return (side + 1 - step // half) % 2 * half + (place + half - 1 - step % half) % half

    load_lat = pltpu.make_async_copy(latent_hbm.at[0], lat, load_sem.at[0])
    load_wqs = pltpu.make_async_copy(wqs_hbm, wqs, load_sem.at[1])
    load_wos = pltpu.make_async_copy(wos_hbm, wos, load_sem.at[2])
    load_wqt = pltpu.make_async_copy(wqt_hbm, wqt, load_sem.at[3])
    load_wot = pltpu.make_async_copy(wot_hbm, wot, load_sem.at[4])
    load_lat.start()
    load_wqs.start()

    barrier = pltpu.get_barrier_semaphore()

    def greet(i, _):
        pl.semaphore_signal(
            barrier, inc=1, device_id={"seq": (me + 1 + i) % n}, device_id_type=pl.DeviceIdType.MESH
        )
        return 0

    lax.fori_loop(0, n - 1, greet, 0)

    attn[...] = jnp.zeros_like(attn)
    v[:, :, hd:padded] = jnp.zeros((n, pos, padded - hd), bf16)
    row_at = lax.broadcasted_iota(jnp.int32, (keys, keys), 0) % GROUP
    col_at = lax.broadcasted_iota(jnp.int32, (keys, keys), 1) % GROUP
    bias[...] = jnp.where(row_at == col_at, 0.0, FAR).astype(f32)

    def project(block, mixed, weights):
        triple = jnp.dot(mixed, weights[...], preferred_element_type=f32)
        at = pl.ds(block * per, per)
        lead = hd - hd % LANES
        key_part = pltpu.roll(triple[:, lead : lead + padded], padded - (hd - lead), 1)
        q[at] = triple[:, :padded].astype(bf16).reshape(per, pos, padded)
        k[at] = key_part.astype(bf16).reshape(per, pos, padded)
        v[at, :, 0:hd] = triple[:, 2 * hd : 3 * hd].astype(bf16).reshape(per, pos, hd)

    def attend(queries, keys_of, values_of, add):
        for base, wide, offset in windows(padded):
            lane = lax.broadcasted_iota(jnp.int32, (1, wide), 1)
            inside = (lane >= offset) & (lane < offset + HEAD_DIM)
            only = inside.astype(f32).astype(bf16)
            scores = lax.dot_general(
                queries(base, wide) * only,
                keys_of(base, wide),
                (((1,), (1,)), ((), ())),
                preferred_element_type=f32,
            )
            if add is not None:
                scores = scores + add
            top = jnp.max(scores, -1, keepdims=True)
            expo = jnp.exp2((scores - top) * factor)
            total = jnp.sum(expo, -1, keepdims=True)
            mixture = jnp.dot(expo.astype(bf16), values_of(base, wide), preferred_element_type=f32)
            rows = mixture.shape[0]
            at = (slice(0, rows), slice(base, base + wide))
            attn[at] = jnp.where(inside, mixture * (1.0 / total), attn[at])

    load_lat.wait()
    load_wqs.wait()
    load_wos.start()
    load_wqt.start()
    load_wot.start()

    def space_project(block, _):
        rows = lat[pl.ds(pl.multiple_of(block * TILE, TILE), TILE), :].astype(f32)
        project(block, modulated(rows, mod[0:1], mod[1:2]), wqs)
        return 0

    lax.fori_loop(0, blocks, space_project, 0)
    load_wos.wait()
    pl.semaphore_wait(barrier, n - 1)

    def forward(to):
        rows = pl.ds(pl.multiple_of(to * pos, pos), pos)
        return pltpu.make_async_remote_copy(
            src_ref=after.at[rows, :],
            dst_ref=recv.at[me],
            send_sem=send_sem.at[to],
            recv_sem=recv_sem.at[me],
            device_id={"seq": to},
            device_id_type=pl.DeviceIdType.MESH,
        )

    def arrival(source):
        return pltpu.make_async_remote_copy(
            src_ref=after.at[pl.ds(0, pos), :],
            dst_ref=recv.at[source],
            send_sem=send_sem.at[source],
            recv_sem=recv_sem.at[source],
            device_id={"seq": source},
            device_id_type=pl.DeviceIdType.MESH,
        )

    def space_attend(step, _):
        block = block_at(step)
        at = pl.ds(block * per, per)
        attend(
            lambda base, wide: q[at, :, base : base + wide].reshape(TILE, wide),
            lambda base, wide: k[:, :, base : base + wide].reshape(tokens, wide),
            lambda base, wide: v[:, :, base : base + wide].reshape(tokens, wide),
            None,
        )
        rows = pl.ds(pl.multiple_of(block * TILE, TILE), TILE)
        delta = jnp.dot(attn[0:TILE, 0:hd].astype(bf16), wos[...], preferred_element_type=f32)
        after[rows, :] = (lat[rows, :].astype(f32) + mod[2:3] * delta).astype(bf16)
        for j in range(per):
            to = block * per + j

            @pl.when(to != me)
            def _():
                forward(to).start()

            @pl.when(to == me)
            def _():
                recv[me] = after[pl.ds(pl.multiple_of(to * pos, pos), pos), :]

        return 0

    lax.fori_loop(0, blocks, space_attend, 0)

    load_wqt.wait()
    load_wot.wait()

    def time_project(step, _):
        block = block_at(step)
        for j in range(per):
            source = block * per + j

            @pl.when(source != me)
            def _():
                arrival(source).wait_recv()

        rows = recv[pl.ds(block * per, per)].reshape(TILE, width).astype(f32)
        project(block, modulated(rows, mod[3:4], mod[4:5]), wqt)
        return 0

    lax.fori_loop(0, blocks, time_project, 0)

    def give_back(to, group):
        at = pl.ds(pl.multiple_of(group * GROUP, GROUP), GROUP)
        return pltpu.make_async_remote_copy(
            src_ref=back_send.at[to, at, :],
            dst_ref=back_recv.at[me, at, :],
            send_sem=bsend_sem.at[group, to],
            recv_sem=brecv_sem.at[group, me],
            device_id={"seq": to},
            device_id_type=pl.DeviceIdType.MESH,
        )

    def returned(source, group):
        at = pl.ds(pl.multiple_of(group * GROUP, GROUP), GROUP)
        return pltpu.make_async_remote_copy(
            src_ref=back_send.at[source, at, :],
            dst_ref=back_recv.at[source, at, :],
            send_sem=bsend_sem.at[group, source],
            recv_sem=brecv_sem.at[group, source],
            device_id={"seq": source},
            device_id_type=pl.DeviceIdType.MESH,
        )

    def time_attend(group, _):
        at = pl.ds(pl.multiple_of(group * GROUP, GROUP), GROUP)

        def rows_of(ref):
            return lambda base, wide: ref[:, at, base : base + wide].reshape(keys, wide)

        attend(rows_of(q), rows_of(k), rows_of(v), bias[...])
        back_send[:, at, :] = attn[0:keys, :].astype(bf16).reshape(n, GROUP, padded)
        back_recv[me, at, :] = back_send[me, at, :]

        def send(i, _):
            give_back((me + n // 2 + i) % n, group).start()
            return 0

        lax.fori_loop(0, n // 2, send, 0)
        lax.fori_loop(n // 2 + 1, n, send, 0)
        return 0

    lax.fori_loop(0, groups, time_attend, 0)

    def store(block):
        rows = pl.ds(pl.multiple_of(block * TILE, TILE), TILE)
        return pltpu.make_async_copy(out.at[rows, :], out_hbm.at[0, rows, :], store_sem.at[block])

    def finish(step, _):
        block = block_at(step)

        def wait_for(i, _):
            source = block * per + i // groups

            @pl.when(source != me)
            def _():
                returned(source, i % groups).wait_recv()

            return 0

        lax.fori_loop(0, per * groups, wait_for, 0)
        rows = pl.ds(pl.multiple_of(block * TILE, TILE), TILE)
        back = back_recv[pl.ds(block * per, per), :, 0:hd].reshape(TILE, hd)
        delta = jnp.dot(back, wot[...], preferred_element_type=f32)
        out[rows, :] = (after[rows, :].astype(f32) + mod[5:6] * delta).astype(bf16)
        store(block).start()
        return 0

    lax.fori_loop(0, blocks, finish, 0)

    def drain(i, _):
        to = (me + 1 + i) % n
        forward(to).wait_send()

        def drain_back(group, _):
            give_back(to, group).wait_send()
            return 0

        lax.fori_loop(0, groups, drain_back, 0)
        return 0

    lax.fori_loop(0, n - 1, drain, 0)

    def stored(block, _):
        store(block).wait()
        return 0

    lax.fori_loop(0, blocks, stored, 0)


def solution(mesh):
    n = mesh.shape["seq"]

    def step(latent, w_qkv_space, w_out_space, w_qkv_time, w_out_time, modulation):
        _, tokens, width = latent.shape
        pos = tokens // n
        hd = HEADS * HEAD_DIM
        padded = -(-hd // LANES) * LANES
        groups = pos // GROUP
        any_space = pl.BlockSpec(memory_space=pl.ANY)
        vmem = pltpu.VMEM
        dma = pltpu.SemaphoreType.DMA
        return pl.pallas_call(
            functools.partial(kernel, n),
            out_shape=jax.ShapeDtypeStruct(latent.shape, bf16),
            in_specs=[any_space] * 5 + [pl.BlockSpec(memory_space=pltpu.VMEM)],
            out_specs=any_space,
            scratch_shapes=[
                vmem((tokens, width), bf16),
                vmem(w_qkv_space.shape, bf16),
                vmem(w_out_space.shape, bf16),
                vmem(w_qkv_time.shape, bf16),
                vmem(w_out_time.shape, bf16),
                vmem((n, pos, padded), bf16),
                vmem((n, pos, padded), bf16),
                vmem((n, pos, padded), bf16),
                vmem((max(TILE, n * GROUP), padded), f32),
                vmem((tokens, width), bf16),
                vmem((n, pos, width), bf16),
                vmem((n * GROUP, n * GROUP), f32),
                vmem((n, pos, padded), bf16),
                vmem((n, pos, padded), bf16),
                vmem((tokens, width), bf16),
                dma((5,)),
                dma((tokens // TILE,)),
                dma((n,)),
                dma((n,)),
                dma((groups, n)),
                dma((groups, n)),
            ],
            compiler_params=pltpu.CompilerParams(
                collective_id=0, has_side_effects=True, vmem_limit_bytes=60 * 1024 * 1024
            ),
        )(latent, w_qkv_space, w_out_space, w_qkv_time, w_out_time, modulation)

    in_specs = (P(("dp", "seq"), None, None), P(), P(), P(), P(), P("dp", None))
    out_specs = P(("dp", "seq"), None, None)
    return jax.shard_map(step, mesh=mesh, in_specs=in_specs, out_specs=out_specs, check_vma=False)
```

time: 270 us -> 131 us (0.49)
  blocking collectives: 121 us -> 0 us
  Pallas kernels: 0 us -> 115 us
  matrix products: 59.8 us -> 0 us
  local copies, waits for them, and re-layouts: 59.8 us -> 16.2 us
  other arithmetic: 28.2 us -> 0 us
    all_to_all x2 -> x0, blocking collectives: 121 us -> none  [the longest x1 63.4 us: shards(): lax.all_to_all(after_space[None], 'seq', split_axis=1, concat_axis=0, til...]
    pallas_call x0 -> x1, Pallas kernels: none -> 115 us  [step(): pl.pallas_call(functools.partial(kernel, n), out_shape=jax.ShapeDtypeStru...]
    dot_general x7 -> x0, matrix products: 42 us -> none  [the longest x1 12.8 us: attend_space(): jnp.einsum('hst,thd->shd', weights, triple[:, 2], preferred_element_type=...]
    unnamed x17 -> x3, local copies, waits for them, and re-layouts: 34.3 us -> 16.2 us
    sub x1 -> x0, matrix products: 17.8 us -> none  [softmax_weights(): expo = jnp.exp(scores - top_score)]
    unnamed x1 -> x0, other arithmetic: 16.3 us -> none
    reshape x2 -> x0, local copies, waits for them, and re-layouts: 12.5 us -> none  [the longest x1 9.93 us: shards(): triple = triple.reshape(frames, positions, 3, HEADS, HEAD_DIM)]
    slice x1 -> x0, local copies, waits for them, and re-layouts: 6.75 us -> none  [shards(): outputs = attend_time(triple[:, :, 0], triple[:, :, 1], triple[:, :, 2])]
where the time goes in v1:
time: 131 us
  Pallas kernels  115 us (88%)
  local copies, waits for them, and re-layouts  16.2 us (12%)
    pallas_call x1, Pallas kernels, step(): pl.pallas_call(functools.partial(kernel, n), out_shape=jax.ShapeDtypeStru...  115 us
    unnamed x3, local copies, waits for them, and re-layouts  16.2 us

profile of v1, /device:TPU:0, one launch (start us, length us, event | category | flops | bytes accessed | tf_op | source)
XLA Modules:
  0.0 131.0 jit_solution(10423736716461180441)
XLA Ops:
  0.0 6.4 %copy.7.wqs_hbm = bf16[1152,1728]{1,0:T(8,128)(2,1)} copy(bf16[1152,1728]{0,1:T(8,128)(2,1)} %param.7) | data formatting | bytes 7962624 | tf_op args[1]
  6.4 6.5 %copy.8.wqt_hbm = bf16[1152,1728]{1,0:T(8,128)(2,1)} copy(bf16[1152,1728]{0,1:T(8,128)(2,1)} %param.9) | data formatting | bytes 7962624 | tf_op args[3]
  12.9 114.9 %shard_map.64 = bf16[1,1024,1152]{2,1,0:T(8,128)(2,1)} custom-call(bf16[1,1024,1152]{2,1,0:T(8,128)(2,1)} %latent_hbm.1, bf16[1152,1728]{1,0:T(8,128)(2,1)} %copy.7.wqs_hbm, bf16[576,1152]{1,0:T(8,128)(2,1)} %wos_hbm.1, bf16[1152,1728]{1,0:T(8,128)(2,1)} %copy.8.wqt_hbm, bf16[576,1152]{1,0:T(8,128)(2,1)} %wot_hbm.1, f32[6,1152]{1,0:T(8,128)} %mod.1), custom_call_target="tpu_custom_call" | custom-call | tf_op jit(solution)/shard_map/pallas_call | solution.py:297
  127.8 3.3 %copy.10 = bf16[1,1024,1152]{2,1,0:T(8,128)(2,1)} copy(bf16[1,1024,1152]{2,1,0:T(8,128)(2,1)} %shard_map.64) | data formatting | bytes 4718592
